TPU v7x, 32 devices: a whole 2x2x4 slice. The times are simulated.
32 devices in a mesh: rows: 8 (over z, y), cols: 4 (over x, core).
Axes of the slice: x: 2, y: 2, z: 4, core: 2. Of those that a mesh axis runs over, the one named last changes fastest.
Arguments:
- latent: bfloat16 [4, 8, 1024], P(None, 'rows', 'cols'), may hold values from -18 to 18
- deep: bfloat16 [320, 8, 1024], P(None, 'rows', 'cols'), may hold values from -6 to 6
- timestep: int32 [1], replicated, may hold values from 0 to 999
- in_weight: bfloat16 [36, 320], replicated, may hold values from -1 to 1
- front_weight: bfloat16 [5760, 320], P('rows'), may hold values from -0.078125 to 0.078125
- middle_weight: bfloat16 [2880, 320], P('cols'), may hold values from -0.109375 to 0.109375
- skip_weight: bfloat16 [640, 320], P('cols'), may hold values from -0.25 to 0.25
- out_weight: bfloat16 [2880, 4], replicated, may hold values from -0.109375 to 0.109375
- time_weight: bfloat16 [320, 1280], replicated, may hold values from -0.3125 to 0.3125
- time_second: bfloat16 [1280, 1280], P('cols'), may hold values from -0.15625 to 0.15625
- time_proj: bfloat16 [1280, 320], replicated, may hold values from -0.15625 to 0.15625
- input_gain: float32 [640], replicated, may hold values from 0.1 to 1.9
- middle_gain: float32 [320], replicated, may hold values from 0.1 to 1.9
- output_gain: float32 [320], replicated, may hold values from 0.1 to 1.9
Outputs:
- noise: float32 [4, 8, 1024], P(None, 'rows', 'cols')
All inputs are finite; a program needn't handle non-finite values.
Results may differ from a plain program's by a relative error of at most 0.0047.
Values may be sent and summed in bfloat16 or wider, within the bound.
A program may use at most 64 MiB of HBM per device.

v0:
```python
import functools
import math

import jax
import jax.numpy as jnp
from jax import lax
from jax.experimental import pallas as pl
from jax.experimental.pallas import tpu as pltpu
from jax.sharding import PartitionSpec as P

GROUPS = 32
EPS = 1e-05
TILE = 16
LANES = 128
MESH = pl.DeviceIdType.MESH
F32 = jnp.float32
BF16 = jnp.bfloat16
SIDES = tuple((i, j) for i in (-1, 0, 1) for j in (-1, 0, 1) if (i, j) != (0, 0))


def dot(a, b, precision=None):
    return lax.dot_general(
        a, b, (((1,), (0,)), ((), ())), preferred_element_type=F32, precision=precision
    )


def split_dot(row, weight):
    high = row.astype(BF16)
    rest = row - high.astype(F32)
    middle = rest.astype(BF16)
    low = (rest - middle.astype(F32)).astype(BF16)
    pieces = jnp.concatenate([high.astype(F32), middle.astype(F32), low.astype(F32)], axis=0)
    return jnp.sum(dot(pieces.astype(BF16), weight), axis=0, keepdims=True)


def silu(z):
    return z / (1.0 + jnp.exp(-z))


def kernel(
    R, Q, ring,
    latent, deep, rows_in, in_w, front, middle, skip, out_w, time_w, time_s, time_p,
    noise,
    lat, jext, hext, oext, shifted, patch, fw, mw, sw, part, emb, sums_a, sums_b,
    lat_s, lat_r, halo_s, halo_r, fz_s, fy_s, fc_s, fm_r, fo_r, mid_s, mid_r, emb_s, emb_r,
    ca_s, ca_r, cb_s, cb_r, loc_s,
):
    r = lax.axis_index("rows")
    c = lax.axis_index("cols")
    C, px = deep.shape
    cin = latent.shape[0]
    image = float(px * R * Q)
    FQ = time_w.shape[0]
    gain_one = rows_in[:, FQ : FQ + 2 * C]
    gain_two = rows_in[:, FQ + 2 * C : FQ + 3 * C]
    gain_three = rows_in[:, FQ + 3 * C : FQ + 4 * C]

    def remote(src, dst, ssem, rsem, rr, cc):
        return pltpu.make_async_remote_copy(
            src_ref=src, dst_ref=dst, send_sem=ssem, recv_sem=rsem,
            device_id={"rows": rr, "cols": cc}, device_id_type=MESH,
        )

    def each(count, body):
        if count <= 8:
            for i in range(1, count):
                body(i)
        else:
            lax.fori_loop(1, count, lambda i, u: (body(i), u)[1], 0)

    barrier = pltpu.get_barrier_semaphore()

    def greet(rr, cc):
        pl.semaphore_signal(barrier, inc=1, device_id={"rows": rr, "cols": cc}, device_id_type=MESH)

    each(R, lambda i: greet(lax.rem(r + i, R), c))
    each(Q, lambda i: greet(r, lax.rem(c + i, Q)))
    for i in (-1, 1):
        for j in (-1, 1):
            greet(lax.rem(r + i + R, R), lax.rem(c + j + Q, Q))
    pl.semaphore_wait(barrier, R - 1 + Q - 1 + 4)

    def inside(rr, cc):
        return (rr >= 0) & (rr < R) & (cc >= 0) & (cc < Q)

    def lat_copy(k, rr, cc):
        i, j = SIDES[k]
        return remote(latent, lat.at[k], lat_s.at[k], lat_r.at[k], rr, cc)

    for k, (i, j) in enumerate(SIDES):
        @pl.when(inside(r + i, c + j))
        def _():
            lat_copy(k, r + i, c + j).start()

        @pl.when(jnp.logical_not(inside(r - i, c - j)))
        def _():
            lat[k] = jnp.zeros(lat.shape[1:], lat.dtype)

    parity = lax.rem(c, 2)
    mate = c + 1 - 2 * parity
    over = lax.rem(c + 2, Q)
    half_c = lax.rem(r, 2)
    twin = r + 1 - 2 * half_c
    mk, sk = middle.shape[0], skip.shape[0]

    def mid_copies(owner, s, slot_from, target):
        rows_m = pl.ds(pl.multiple_of(owner * mk, TILE), mk)
        rows_s = pl.ds(pl.multiple_of(owner * sk, TILE), sk)
        src_m, src_s = (middle, skip) if slot_from else (mw.at[rows_m], sw.at[rows_s])
        return (
            remote(src_m, mw.at[rows_m], mid_s.at[0, s], mid_r.at[0, s], r, target),
            remote(src_s, sw.at[rows_s], mid_s.at[1, s], mid_r.at[1, s], r, target),
        )

    fk = fw.shape[0] // R if ring else 0
    cut = fk // 2 // TILE * TILE
    spans = ((0, cut), (cut, fk - cut))

    def f_rows(owner, par):
        return pl.ds(pl.multiple_of(owner * fk, TILE) + spans[par][0], spans[par][1])

    def by_parity(par_of, body):
        for par in (0, 1):
            @pl.when(par_of == par)
            def _():
                body(par)

    def f_own(par, target, ssem):
        src = front.at[pl.ds(spans[par][0], spans[par][1])]
        return remote(src, fw.at[f_rows(r, par)], ssem, fm_r.at[r], target, c)

    def f_pass(owner, par, target):
        return remote(fw.at[f_rows(owner, par)], fw.at[f_rows(owner, par)],
                      fy_s.at[owner], fm_r.at[owner], target, c)

    def f_mate(owner, par):
        return remote(fw.at[f_rows(owner, par)], fw.at[f_rows(owner, par)],
                      fc_s.at[owner], fo_r.at[owner], r, mate)

    def by_distance(distances, body):
        for d in distances:
            for t in (r + 2 * d, r - 2 * d):
                @pl.when((t >= 0) & (t < R))
                def _():
                    body(t)

    locals_ = []
    if ring:
        locals_.append(pltpu.make_async_copy(
            front, fw.at[pl.ds(pl.multiple_of(r * fk, TILE), fk)], loc_s.at[0]))
    locals_.append(pltpu.make_async_copy(
        middle, mw.at[pl.ds(pl.multiple_of(c * mk, TILE), mk)], loc_s.at[1]))
    locals_.append(pltpu.make_async_copy(
        skip, sw.at[pl.ds(pl.multiple_of(c * sk, TILE), sk)], loc_s.at[2]))
    for copy in locals_:
        copy.start()

    if ring:
        def first(par):
            f_own(par, twin, fy_s.at[r]).start()
            def one(t):
                f_own(par, t, fz_s.at[t]).start()
            by_distance(range(1, R // 2), one)
        by_parity(parity, first)
    for copy in mid_copies(c, 0, True, over) + mid_copies(c, 1, True, mate):
        copy.start()

    def pass_on(distances):
        def go(par):
            def one(owner):
                f_pass(owner, par, twin).wait_recv()
                f_pass(owner, par, twin).start()
                f_mate(owner, par).start()
            by_distance(distances, one)
        by_parity(parity, go)

    for k, (i, j) in enumerate(SIDES):
        @pl.when(inside(r - i, c - j))
        def _():
            lat_copy(k, r - i, c - j).wait_recv()
    where = {side: k for k, side in enumerate(SIDES)}
    for a in range(3):
        tiles = []
        for b in range(3):
            side = (1 - a, 1 - b)
            block = latent[...] if side == (0, 0) else lat[where[side]]
            tiles.append(block.astype(F32))
        wide = jnp.concatenate(tiles, axis=1)
        for b in range(3):
            start = px + b - 1
            patch[cin * (3 * a + b) : cin * (3 * a + b + 1), :] = wide[:, start : start + px]
    skip_feat = dot(patch[...].T.astype(BF16), in_w[...]).astype(BF16)
    deep_t = deep[...].astype(F32).T.astype(BF16)
    own = pl.ds(TILE, px)
    jext[1, own, :] = jnp.concatenate([deep_t.astype(F32), skip_feat.astype(F32)], axis=1).astype(BF16)

    def halo_copy(stage, ext, k, rr, cc):
        i, j = SIDES[k]
        src = ((TILE, TILE), (TILE, px), (px, TILE))[j + 1]
        dst = ((TILE + px, TILE), (TILE, px), (0, TILE))[j + 1]
        return remote(ext.at[1, pl.ds(*src), :], ext.at[1 - i, pl.ds(*dst), :],
                      halo_s.at[stage, k], halo_r.at[stage, k], rr, cc)

    def halo_send(stage, ext):
        for k, (i, j) in enumerate(SIDES):
            @pl.when(inside(r + i, c + j))
            def _():
                halo_copy(stage, ext, k, r + i, c + j).start()

            @pl.when(jnp.logical_not(inside(r - i, c - j)))
            def _():
                dst = ((TILE + px, TILE), (TILE, px), (0, TILE))[j + 1]
                ext[1 - i, pl.ds(*dst), :] = jnp.zeros((dst[1], ext.shape[2]), ext.dtype)

    def halo_wait(stage, ext):
        for k, (i, j) in enumerate(SIDES):
            @pl.when(inside(r - i, c - j))
            def _():
                halo_copy(stage, ext, k, r - i, c - j).wait_recv()

    def indicator(channels, flip):
        shape = (LANES, channels) if flip else (channels, LANES)
        size = channels // GROUPS
        ch = lax.broadcasted_iota(jnp.int32, shape, 1 if flip else 0)
        g = lax.broadcasted_iota(jnp.int32, shape, 0 if flip else 1)
        return ((ch >= g * size) & (ch < g * size + size)).astype(F32)

    def sum_copy(buf, ssem, rsem, stage, slot, i, rr, cc):
        return remote(buf.at[stage, slot], buf.at[stage, slot],
                      ssem.at[stage, i], rsem.at[stage, i], rr, cc)

    def reduce_start(stage, values):
        top = jnp.sum(values, axis=0, keepdims=True)
        low = jnp.sum(values * values, axis=0, keepdims=True)
        both = jnp.concatenate([top, low, jnp.zeros((6, values.shape[1]), F32)], axis=0)
        sums_a[stage, c] = dot(both, indicator(values.shape[1], False), lax.Precision.HIGHEST)
        for i in range(1, Q):
            sum_copy(sums_a, ca_s, ca_r, stage, c, i, r, lax.rem(c + i, Q)).start()

    def reduce_end(stage, channels):
        for i in range(1, Q):
            s = lax.rem(c + Q - i, Q)
            sum_copy(sums_a, ca_s, ca_r, stage, s, i, r, s).wait_recv()
        sums_b[stage, r] = jnp.sum(sums_a[stage], axis=0)
        each(R, lambda i: sum_copy(sums_b, cb_s, cb_r, stage, r, i, lax.rem(r + i, R), c).start())

        def got(i):
            s = lax.rem(r + R - i, R)
            sum_copy(sums_b, cb_s, cb_r, stage, s, i, s, c).wait_recv()

        each(R, got)
        total = jnp.sum(sums_b[stage], axis=0) / (channels // GROUPS * image)
        center = total[0:1]
        inverse = lax.rsqrt(total[1:2] - center * center + EPS)
        both = jnp.concatenate([center, inverse, jnp.zeros((6, LANES), F32)], axis=0)
        wide = dot(both, indicator(channels, True), lax.Precision.HIGHEST)
        return wide[0:1], wide[1:2]

    def conv(ext, stats, gain, weight, exact=None, shift=None):
        center, inverse = stats
        if shift is not None:
            center = center - shift
        channels = ext.shape[2]
        scale = inverse * gain
        place = lax.broadcasted_iota(jnp.int32, (px + 2 * TILE, 1), 0)
        inner = (place >= TILE) & (place < TILE + px)
        total = None
        for a in (1, 0, 2):
            z = (ext[a].astype(F32) - center) * scale
            here = r + a - 1
            keep = (here >= 0) & (here < R) & (
                inner | ((place < TILE) & (c > 0)) | ((place >= TILE + px) & (c < Q - 1)))
            shifted[:, 0:channels] = jnp.where(keep, silu(z), 0.0)
            if a == 1 and exact is not None:
                shifted[own, 0:channels] = silu((exact - center) * scale)
            for b in range(3):
                act = shifted[TILE + b - 1 : TILE + b - 1 + px, 0:channels].astype(BF16)
                k = (3 * a + b) * channels
                term = dot(act, weight[k : k + channels, :])
                total = term if total is None else total + term
        return total

    joined = jext[1, own, :]
    reduce_start(0, joined.astype(F32))
    halo_send(0, jext)

    hidden = silu(split_dot(rows_in[:, 0:FQ], time_w[...]))
    tk = time_s.shape[0]
    for q in range(Q):
        @pl.when(c == q)
        def _():
            part[...] = hidden[:, q * tk : (q + 1) * tk]
    emb_own = split_dot(part[...], time_s[...])
    emb[c] = emb_own

    def emb_copy(i, src_c, tgt):
        return remote(emb.at[src_c], emb.at[src_c], emb_s.at[i], emb_r.at[i], r, tgt)

    for i in range(1, Q):
        emb_copy(i, c, lax.rem(c + i, Q)).start()

    if ring:
        pass_on((1,))
    stats = reduce_end(0, 2 * C)
    if ring:
        pass_on(range(2, R // 2))

        def from_twin(par):
            def one(t):
                owner = t + twin - r
                f_pass(owner, par, twin).wait_recv()
                f_mate(owner, par).start()
            one(r)
            by_distance(range(1, R // 2), one)
        by_parity(parity, from_twin)

    for copy in mid_copies(over, 0, False, over):
        copy.wait_recv()
    for copy in mid_copies(over, 2, False, mate):
        copy.start()

    for i in range(1, Q):
        s = lax.rem(c + Q - i, Q)
        emb_copy(i, s, s).wait_recv()
    embedded = jnp.sum(emb[...], axis=0)
    time_shift = split_dot(silu(embedded), time_p[...])

    for copy in locals_:
        copy.wait()
    halo_wait(0, jext)
    if ring:
        def from_mate(i):
            owner = lax.rem(r + i, R)
            def go(par):
                f_mate(owner, 1 - par).wait_recv()
            by_parity(parity, go)
        for i in range(1, R):
            from_mate(i)
    front_out = conv(jext, stats, gain_one, fw if ring else front)

    hext[1, own, :] = front_out.astype(BF16)
    reduce_start(1, front_out + time_shift)
    halo_send(1, hext)
    for copy in mid_copies(mate, 1, False, mate):
        copy.wait_recv()
    far = lax.rem(mate + 2, Q)
    for copy in mid_copies(far, 2, False, mate):
        copy.wait_recv()
    shortcut = dot(joined, sw[...])
    stats = reduce_end(1, C)
    halo_wait(1, hext)
    block_out = conv(hext, stats, gain_two, mw, front_out, time_shift) + shortcut

    oext[1, own, :] = block_out.astype(BF16)
    reduce_start(2, block_out)
    halo_send(2, oext)
    stats = reduce_end(2, C)
    halo_wait(2, oext)
    result = conv(oext, stats, gain_three, out_w, block_out)
    noise[...] = result.T[0 : noise.shape[0], :]

    for k, (i, j) in enumerate(SIDES):
        @pl.when(inside(r + i, c + j))
        def _():
            lat_copy(k, r + i, c + j).wait_send()
            for stage, ext in enumerate((jext, hext, oext)):
                halo_copy(stage, ext, k, r + i, c + j).wait_send()
    for i in range(1, Q):
        emb_copy(i, c, lax.rem(c + i, Q)).wait_send()
        for stage in range(3):
            sum_copy(sums_a, ca_s, ca_r, stage, c, i, r, lax.rem(c + i, Q)).wait_send()

    def sent(i):
        for stage in range(3):
            sum_copy(sums_b, cb_s, cb_r, stage, r, i, lax.rem(r + i, R), c).wait_send()

    each(R, sent)
    for copy in (mid_copies(c, 0, True, over) + mid_copies(c, 1, True, mate)
                 + mid_copies(over, 2, False, mate)):
        copy.wait_send()
    if ring:
        def last(par):
            f_own(par, twin, fy_s.at[r]).wait_send()
            def one(t):
                f_own(par, t, fz_s.at[t]).wait_send()
                f_pass(t, par, twin).wait_send()
            by_distance(range(1, R // 2), one)
            for i in range(1, R):
                f_mate(lax.rem(r + i, R), par).wait_send()
        by_parity(parity, last)


def shards(
    R, Q,
    latent, deep, timestep, in_weight, front_weight, middle_weight, skip_weight, out_weight,
    time_weight, time_second, time_proj, input_gain, middle_gain, output_gain,
):
    C = deep.shape[0]
    cin = latent.shape[0]
    px = deep.shape[1] * deep.shape[2]
    assert deep.shape[1] == 1 and Q == 4 and R % 2 == 0 and R > 2
    ring = R <= 8 and front_weight.shape[0] % TILE == 0
    half = time_weight.shape[0] // 2
    ratios = jnp.exp(-math.log(10000.0) * jnp.arange(half, dtype=F32) / half)
    angles = timestep[0].astype(F32) * ratios
    rows_in = jnp.concatenate(
        [jnp.cos(angles), jnp.sin(angles), input_gain, middle_gain, output_gain])[None, :]
    front = front_weight if ring else lax.all_gather(front_weight, "rows", axis=0, tiled=True)
    couts = out_weight.shape[1]
    out_w = jnp.pad(out_weight, ((0, 0), (0, LANES - couts)))
    vmem = pl.BlockSpec(memory_space=pltpu.VMEM)
    dma = pltpu.SemaphoreType.DMA
    wide = time_second.shape[1]
    tall = px + 2 * TILE
    args = (
        latent.reshape(cin, px), deep.reshape(C, px), rows_in, in_weight, front,
        middle_weight, skip_weight, out_w, time_weight, time_second, time_proj,
    )
    out = pl.pallas_call(
        functools.partial(kernel, R, Q, ring),
        out_shape=jax.ShapeDtypeStruct((couts, px), F32),
        in_specs=[vmem] * len(args),
        out_specs=vmem,
        scratch_shapes=[
            pltpu.VMEM((8, cin, px), BF16),
            pltpu.VMEM((3, tall, 2 * C), BF16),
            pltpu.VMEM((3, tall, C), BF16),
            pltpu.VMEM((3, tall, C), BF16),
            pltpu.VMEM((tall, 2 * C), F32),
            pltpu.VMEM((9 * cin, px), F32),
            pltpu.VMEM((18 * C if ring else TILE, C), BF16),
            pltpu.VMEM((9 * C, C), BF16),
            pltpu.VMEM((2 * C, C), BF16),
            pltpu.VMEM((1, time_second.shape[0]), F32),
            pltpu.VMEM((Q, 1, wide), F32),
            pltpu.VMEM((3, Q, 8, LANES), F32),
            pltpu.VMEM((3, R, 8, LANES), F32),
            dma((8,)), dma((8,)), dma((3, 8)), dma((3, 8)),
            dma((R,)), dma((R,)), dma((R,)), dma((R,)), dma((R,)),
            dma((2, 3)), dma((2, 3)), dma((Q,)), dma((Q,)),
            dma((3, Q)), dma((3, Q)), dma((3, R)), dma((3, R)), dma((3,)),
        ],
        compiler_params=pltpu.CompilerParams(
            collective_id=0, has_side_effects=True, vmem_limit_bytes=56 * 1024 * 1024
        ),
    )(*args)
    return out.reshape(couts, 1, px)


UNIT = 16
PACK = 24
ALONE = 3


class Box:
    pass


def snake(pos, c, R):
    q = pos + lax.rem(c, 2) * (R - 1 - 2 * pos)
    late = q // (R // 2)
    return (1 - late) * (2 * q) + late * (2 * (R - 1 - q) + 1)


def place_of(r, c, R):
    odd, h = lax.rem(r, 2), r // 2
    q = (1 - odd) * h + odd * (R - 1 - h)
    return q + lax.rem(c, 2) * (R - 1 - 2 * q)


def dot_nt(a, b, precision=None):
    return lax.dot_general(
        a, b, (((1,), (1,)), ((), ())), preferred_element_type=F32, precision=precision
    )


def pieces_of(row):
    high = row.astype(BF16)
    rest = row - high.astype(F32)
    middle = rest.astype(BF16)
    low = (rest - middle.astype(F32)).astype(BF16)
    return jnp.concatenate(
        [high.astype(F32), middle.astype(F32), low.astype(F32)], axis=0).astype(BF16)


def fast_kernel(
    R, Q, names,
    latent, deep, timestep, in_w, front, middle, skip, out_w, time_w, time_s, time_p,
    input_gain, middle_gain, output_gain, noise, *scratch,
):
    v = Box()
    for name, ref in zip(names, scratch):
        setattr(v, name, ref)
    r = lax.axis_index("rows")
    c = lax.axis_index("cols")
    C, px = deep.shape
    cin = latent.shape[0]
    couts = out_w.shape[0]
    image = float(px * R * Q)
    FQ = time_w.shape[0]
    W = px // R
    N = W * 8
    s = place_of(r, c, R)
    me = c * R + r
    CP = (C + LANES - 1) // LANES * LANES
    GAP = CP - C

    def remote(src, dst, ssem, rsem, rr, cc):
        return pltpu.make_async_remote_copy(
            src_ref=src, dst_ref=dst, send_sem=ssem, recv_sem=rsem,
            device_id={"rows": rr, "cols": cc}, device_id_type=MESH,
        )

    others = [(i, j) for i in range(R) for j in range(Q) if (i, j) != (0, 0)]
    barrier = pltpu.get_barrier_semaphore()
    for i, j in others:
        pl.semaphore_signal(
            barrier, inc=1, device_id={"rows": lax.rem(r + i, R), "cols": lax.rem(c + j, Q)},
            device_id_type=MESH)

    mk, skr, fk = middle.shape[1], skip.shape[0], front.shape[1]
    loads = {}
    for k, (name, src, dst) in enumerate((
        ("deep", deep, v.deep_v), ("front", front, v.front_v), ("latent", latent, v.lat_v),
        ("in", in_w, v.inw), ("tw", time_w, v.tw), ("ts", time_s, v.ts),
        ("middle", middle, v.mid_v),
        ("skip", skip, v.sw.at[pl.ds(pl.multiple_of(c * skr, TILE), skr)]),
        ("tp", time_p, v.tp), ("out", out_w, v.outw_v),
        ("gain_one", input_gain, v.gain_one), ("gain_two", middle_gain, v.gain_two),
        ("gain_three", output_gain, v.gain_three),
    )):
        loads[name] = pltpu.make_async_copy(src, dst, v.ld_s.at[k])
        loads[name].start()

    loads["deep"].wait()
    deep_t = v.deep_v[...].astype(F32).T
    v.dr[:, C:CP] = jnp.zeros((px, GAP), BF16)
    v.dr[:, 0:C] = deep_t.astype(BF16)
    pad = jnp.zeros((1, GAP), F32)
    deep_top = jnp.concatenate([jnp.sum(deep_t, axis=0, keepdims=True), pad], axis=1)
    deep_low = jnp.concatenate([jnp.sum(deep_t * deep_t, axis=0, keepdims=True), pad], axis=1)
    tall = PACK * UNIT
    main = C // LANES * LANES
    tail = C - main

    def packed(ref, k):
        turned = ref[...].astype(F32).T
        first, second = turned[0:tall], turned[k - tall : k]
        mixed = jnp.concatenate([first[:, main:C], second[:, main:C]], axis=1)
        return jnp.concatenate([first[:, 0:main], mixed, second[:, 0:main]], axis=1).astype(BF16)

    def unpack(block, ref, start):
        mixed = block[:, main : main + LANES]
        ref[start : start + tall, 0:main] = block[:, 0:main]
        ref[start : start + tall, main : main + LANES] = mixed
        swapped = pltpu.roll(mixed.astype(F32), LANES - tail, 1).astype(BF16)
        start = start + fk - tall
        ref[start : start + tall, 0:main] = block[:, main + LANES : 2 * C]
        ref[start : start + tall, main : main + LANES] = swapped

    loads["latent"].wait()
    v.lat[0, r] = v.lat_v[...]
    loads["front"].wait()
    v.fp[r] = packed(v.front_v, fk)

    pl.semaphore_wait(barrier, len(others))

    def lat_row(i, rr):
        return remote(v.lat_v, v.lat.at[0, r], v.one_s.at[0], v.one_r.at[0], rr, c)

    for i in range(1, R):
        lat_row(i, lax.rem(r + i, R)).start()

    def lat_left():
        return remote(v.lat_v, v.lat.at[2, r], v.one_s.at[1], v.one_r.at[2],
                      snake(R - 1, c - 1, R), c - 1)

    def lat_right():
        return remote(v.lat_v, v.lat.at[1, r], v.one_s.at[2], v.one_r.at[1],
                      snake(0, c + 1, R), c + 1)

    @pl.when(c > 0)
    def _():
        lat_left().start()

    @pl.when(c < Q - 1)
    def _():
        lat_right().start()

    core, xx = lax.rem(c, 2), c // 2
    mate = c + 1 - 2 * core
    over = lax.rem(c + 2, Q)
    y = lax.rem(r, 2)
    twin = r + 1 - 2 * y
    share = PACK // 2
    both = (share - 2 * ALONE) // 2
    sizes = {0: ALONE + both, 1: both, "E": ALONE}

    def f_part(owner, part, x_of, core_of):
        first = {
            0: x_of * (ALONE + both), 1: ALONE + both - x_of * both, "E": x_of * (ALONE + 2 * both),
        }[part]
        return v.fp.at[owner, pl.ds(
            pl.multiple_of((core_of * share + first) * UNIT, UNIT), sizes[part] * UNIT)]

    def f_move(owner, part, ssem, rr, cc):
        ref = f_part(owner, part, xx, core)
        return remote(ref, ref, ssem, v.fm_r.at[part, owner], rr, cc)

    def f_up(owner, part):
        return f_move(owner, part, v.one_s.at[6], r + 2, c)

    def f_down(owner, part):
        return f_move(owner, part, v.one_s.at[7], r - 2, c)

    def f_twin(owner, part):
        return f_move(owner, part, v.one_s.at[8], twin, c)

    def f_over(owner, x_of):
        ref = f_part(owner, "E", x_of, core)
        return remote(ref, ref, v.one_s.at[9], v.fx_r.at[owner], r, over)

    def f_mate(owner, part):
        ref = f_part(owner, part, xx, core)
        return remote(ref, ref, v.one_s.at[10], v.one_r.at[10], r, mate)

    def f_mate_extra(owner):
        ref = f_part(owner, "E", 1 - xx, core)
        return remote(ref, ref, v.one_s.at[10], v.one_r.at[10], r, mate)

    def when_row(t, body):
        @pl.when((t >= 0) & (t < R))
        def _():
            body()

    for part in (0, 1):
        when_row(r + 2, lambda: f_up(r, part).start())
        when_row(r - 2, lambda: f_down(r, part).start())
        f_twin(r, part).start()

    def from_z(d, sign, part):
        t = r + sign * 2 * d

        def body():
            f_twin(t, part).wait_recv()
            if sign < 0:
                when_row(r + 2, lambda: f_up(t, part).start())
            else:
                when_row(r - 2, lambda: f_down(t, part).start())
            f_twin(t, part).start()
            if part == 0:
                f_over(t, xx).start()
            f_mate(t, part).start()
        when_row(t, body)

    def from_y(owner, part):
        f_twin(owner, part).wait_recv()
        if part == 0:
            f_over(owner, xx).start()
        f_mate(owner, part).start()

    def z_steps(d):
        for part in (0, 1):
            for sign in (-1, 1):
                from_z(d, sign, part)

    def y_steps(d):
        for part in (0, 1):
            for sign in (-1, 1):
                t = r + sign * 2 * d
                when_row(t, lambda: from_y(t + twin - r, part))

    def a2a_copy(q):
        return remote(v.dr.at[pl.ds(W * q, W)], v.a2a.at[r], v.one_s.at[3], v.one_r.at[3],
                      snake(q, c, R), c)

    for q in range(R):
        @pl.when(s != q)
        def _():
            a2a_copy(q).start()

        @pl.when(s == q)
        def _():
            v.a2a[r] = v.dr[pl.ds(W * q, W), :]

    loads["middle"].wait()
    v.mp[c] = packed(v.mid_v, mk)
    loads["skip"].wait()
    cut_rows = tall // 2

    def mid_half(owner, which):
        return v.mp.at[owner, pl.ds(pl.multiple_of(which * cut_rows, UNIT), cut_rows)]

    def skip_rows(owner):
        return v.sw.at[pl.ds(pl.multiple_of(owner * skr, TILE), skr)]

    def mid_copy(ref, n, rr, cc):
        return remote(ref, ref, v.mid_s.at[n], v.mid_r.at[n], rr, cc)

    mid_over = (mid_copy(mid_half(c, y), 0, r, over), mid_copy(skip_rows(c), 1, r, over))
    mid_over_in = (mid_copy(mid_half(over, y), 0, r, over), mid_copy(skip_rows(over), 1, r, over))
    mid_twin = mid_copy(mid_half(over, y), 2, twin, c)
    mid_twin_in = mid_copy(mid_half(over, 1 - y), 2, twin, c)
    mid_mate = (mid_copy(v.mp.at[c], 3, r, mate), mid_copy(skip_rows(c), 4, r, mate),
                mid_copy(v.mp.at[over], 5, r, mate), mid_copy(skip_rows(over), 6, r, mate))
    far = lax.rem(mate + 2, Q)
    mid_mate_in = (mid_copy(v.mp.at[mate], 3, r, mate), mid_copy(skip_rows(mate), 4, r, mate),
                   mid_copy(v.mp.at[far], 5, r, mate), mid_copy(skip_rows(far), 6, r, mate))
    for copy in mid_over + mid_mate[0:2]:
        copy.start()

    loads["in"].wait()
    inw = v.inw[...].astype(F32)
    v.wb[...] = jnp.zeros(v.wb.shape, F32)
    for b in range(3):
        rows = [inw[cin * (3 * a + b) : cin * (3 * a + b + 1), :] for a in range(3)]
        band = jnp.concatenate(rows, axis=0)
        band = jnp.concatenate([jnp.zeros((3 * cin, GAP), F32), band], axis=1)
        for yy in range(R):
            lo, hi = max(0, yy - 1), min(R, yy + 2)
            v.wb[b, lo * cin : hi * cin, yy * CP : (yy + 1) * CP] = (
                band[(lo - yy + 1) * cin : (hi - yy + 1) * cin, :])

    loads["tw"].wait()
    loads["ts"].wait()
    half = FQ // 2
    index = lax.broadcasted_iota(jnp.int32, (1, half), 1).astype(F32)
    angles = timestep[0].astype(F32) * jnp.exp(-math.log(10000.0) * index / half)
    v.part[:, 0:half] = jnp.cos(angles)
    v.part[:, half:FQ] = jnp.sin(angles)
    hidden = silu(jnp.sum(dot(pieces_of(v.part[...]), v.tw[...]), axis=0, keepdims=True))
    tk = time_s.shape[0]
    for q in range(Q):
        @pl.when(c == q)
        def _():
            v.part[...] = hidden[:, q * tk : (q + 1) * tk]
    v.emb[c] = jnp.sum(dot(pieces_of(v.part[...]), v.ts[...]), axis=0, keepdims=True)

    def emb_copy(i, src_c, target):
        return remote(v.emb.at[src_c], v.emb.at[src_c], v.one_s.at[5], v.one_r.at[5], r, target)

    for i in range(1, Q):
        emb_copy(i, c, lax.rem(c + i, Q)).start()

    @pl.when((s != 0) | (c == 0))
    def _():
        v.lat[1] = jnp.zeros(v.lat.shape[1:], BF16)

    @pl.when((s != R - 1) | (c == Q - 1))
    def _():
        v.lat[2] = jnp.zeros(v.lat.shape[1:], BF16)

    def all_of(ref, n):
        return remote(ref, ref, v.one_s.at[n], v.one_r.at[n], twin, c)

    all_of(v.lat.at[0, pl.ds(0, R - 1)], 0).wait_recv()

    @pl.when((s == 0) & (c > 0))
    def _():
        all_of(v.lat.at[1], 1).wait_recv()

    @pl.when((s == R - 1) & (c < Q - 1))
    def _():
        all_of(v.lat.at[2], 2).wait_recv()

    for k in range(3):
        for q in range(R):
            v.latrows[k, cin * q : cin * (q + 1), :] = v.lat[k, q].astype(F32)
    lane = lax.broadcasted_iota(jnp.int32, (R * cin, px), 1)
    base = jnp.where((lane == px - 1) & (s == 0), v.latrows[1], v.latrows[0])
    base = jnp.where((lane == 0) & (s == R - 1), v.latrows[2], base)
    rolled = pltpu.roll(base, lax.rem(px + 1 - W * s, px), 1)
    v.tap[0:LANES, 0 : R * cin] = rolled[:, 0:LANES].T
    total = None
    for b in range(3):
        term = dot(v.tap[b : b + W, 0 : R * cin].astype(BF16), v.wb[b].astype(BF16))
        total = term if total is None else total + term
    v.sk[...] = total.astype(BF16).astype(F32)
    top = low = None
    for q in range(R):
        slab = v.sk[:, q * CP : (q + 1) * CP]
        top = slab if top is None else top + slab
        low = slab * slab if low is None else low + slab * slab
    skip_top = jnp.sum(top, axis=0, keepdims=True)
    skip_low = jnp.sum(low, axis=0, keepdims=True)

    def join(d, k):
        cut = C // LANES * LANES
        return jnp.concatenate(
            [d[:, 0:cut], d[:, cut:CP] + k[:, 0 : CP - cut], k[:, CP - cut : CP]], axis=1)

    def indicator(channels, flip):
        shape = (LANES, channels) if flip else (channels, LANES)
        size = channels // GROUPS
        ch = lax.broadcasted_iota(jnp.int32, shape, 1 if flip else 0)
        g = lax.broadcasted_iota(jnp.int32, shape, 0 if flip else 1)
        return ((ch >= g * size) & (ch < g * size + size)).astype(F32)

    def sum_copy(stage, slot, i, rr, cc):
        return remote(v.sums.at[stage, slot], v.sums.at[stage, slot],
                      v.sum_s.at[stage], v.sum_r.at[stage], rr, cc)

    def reduce_start(stage, top, low):
        channels = top.shape[1]
        both = jnp.concatenate([top, low, jnp.zeros((6, channels), F32)], axis=0)
        res = dot(both, indicator(channels, False), lax.Precision.HIGHEST)
        v.sums[stage, me] = res[0:1] + pltpu.roll(res, GROUPS, 1)[1:2]
        for n, (i, j) in enumerate(others):
            sum_copy(stage, me, n, lax.rem(r + i, R), lax.rem(c + j, Q)).start()

    def sum_all(stage):
        ref = v.sums.at[stage, pl.ds(0, R * Q - 1)]
        return remote(ref, ref, v.sum_s.at[stage], v.sum_r.at[stage], twin, c)

    def reduce_end(stage, channels):
        sum_all(stage).wait_recv()
        total = jnp.sum(v.sums[stage], axis=0) / (channels // GROUPS * image)
        spread = pltpu.roll(total, LANES - GROUPS, 1) - total * total
        inverse = lax.rsqrt(jnp.maximum(spread, 0.0) + EPS)
        both = jnp.concatenate([total, inverse, jnp.zeros((6, LANES), F32)], axis=0)
        both = jnp.where(lax.broadcasted_iota(jnp.int32, (8, LANES), 1) < GROUPS, both, 0.0)
        wide = dot(both, indicator(channels, True), lax.Precision.HIGHEST)
        return wide[0:1], wide[1:2]

    reduce_start(0, join(deep_top, skip_top), join(deep_low, skip_low))

    inner = (s + R - 1) // R
    last = (s + 1) // R
    left = (inner * snake(s - 1, c, R) + (1 - inner) * r, c - (1 - inner))
    right = ((1 - last) * snake(s + 1, c, R) + last * r, c + last)
    has_left, has_right = left[1] >= 0, right[1] < Q

    def halo_left(stage, ext):
        return remote(ext.at[:, pl.ds(8, 8)], ext.at[:, pl.ds(N + 8, 8)],
                      v.halo_s.at[stage, 0], v.halo_r.at[stage, 1], left[0], left[1])

    def halo_right(stage, ext):
        return remote(ext.at[:, pl.ds(N, 8)], ext.at[:, pl.ds(0, 8)],
                      v.halo_s.at[stage, 1], v.halo_r.at[stage, 0], right[0], right[1])

    def halo_send(stage, ext):
        zeros = jnp.zeros((ext.shape[0], 8, LANES), F32)

        @pl.when(has_left)
        def _():
            halo_left(stage, ext).start()

        @pl.when(has_right)
        def _():
            halo_right(stage, ext).start()

        @pl.when(jnp.logical_not(has_left))
        def _():
            ext[:, 0:8, :] = zeros

        @pl.when(jnp.logical_not(has_right))
        def _():
            ext[:, N + 8 : N + 16, :] = zeros

    def halo_wait(stage, ext):
        @pl.when(has_left)
        def _():
            halo_right(stage, ext).wait_recv()

        @pl.when(has_right)
        def _():
            halo_left(stage, ext).wait_recv()

    z_steps(1)
    for part in (0, 1):
        from_y(twin, part)

    all_of(v.a2a.at[pl.ds(0, R - 1)], 3).wait_recv()
    for q in range(R):
        joined = join(v.a2a[q].astype(F32), v.sk[:, q * CP : (q + 1) * CP])
        for n in range(2 * C // LANES):
            v.jx[n, pl.ds(8 + q, W, 8), :] = joined[:, n * LANES : (n + 1) * LANES]
    halo_send(0, v.jx)
    z_steps(2)
    y_steps(1)
    for d in range(3, R // 2):
        z_steps(d)
        y_steps(d - 1)
    y_steps(R // 2 - 1)
    for copy in mid_over_in:
        copy.wait_recv()
    for copy in (mid_twin, mid_mate[3]):
        copy.start()

    loads["out"].wait()
    loads["tp"].wait()
    for name in ("gain_one", "gain_two", "gain_three"):
        loads[name].wait()
    v.wr32[...] = jnp.zeros(v.wr32.shape, F32)
    for t in range(9):
        v.wr32[couts * t : couts * (t + 1), :] = v.outw_v[:, C * t : C * (t + 1)].astype(F32)
    out_taps = v.wr32[...].T.astype(BF16)

    all_of(v.emb.at[pl.ds(0, Q - 1)], 5).wait_recv()
    embedded = jnp.sum(v.emb[...], axis=0)
    time_shift = jnp.sum(dot_nt(pieces_of(silu(embedded)), v.tp[...]), axis=0, keepdims=True)

    place = lax.broadcasted_iota(jnp.int32, (W + 2, 8, 1), 0)
    inside = (
        ((place > 0) | has_left) & ((place < W + 1) | has_right))
    row = lax.broadcasted_iota(jnp.int32, (W + 2, 8, 1), 1)

    def keep_own(ext, values):
        for n in range(ext.shape[0]):
            lo, hi = n * LANES, min((n + 1) * LANES, values.shape[1])
            ext[n, 8 : N + 8, 0 : hi - lo] = values[:, lo:hi]

    def rows_of(ext, channels, first, count):
        return jnp.concatenate(
            [ext[n, first : first + count, 0 : min(LANES, channels - n * LANES)]
             for n in range(ext.shape[0])], axis=1)

    def activate(ext, stats, gain):
        center, inverse = stats
        scale = inverse * gain
        channels = gain.shape[1]
        for lo in range(0, channels, LANES):
            hi = min(channels, lo + LANES)
            z = silu((ext[lo // LANES, :, 0 : hi - lo] - center[:, lo:hi]) * scale[:, lo:hi])
            z = jnp.where(inside, z.reshape(W + 2, 8, hi - lo), 0.0)
            for a in range(3):
                if a == 1:
                    moved = z
                elif a == 0:
                    moved = jnp.where(row > 0, pltpu.roll(z, 1, 1), 0.0)
                else:
                    moved = jnp.where(row < 7, pltpu.roll(z, 7, 1), 0.0)
                flat = moved.reshape(N + 16, hi - lo)
                v.act_a[a, :, lo:hi] = flat.astype(BF16)
                v.act_b[a, :, lo:hi] = flat[8 : N + 8].astype(BF16)

    def conv(channels, weight):
        total = None
        for a in range(3):
            for b in range(3):
                if b == 1:
                    act = v.act_b[a, :, 0:channels]
                else:
                    act = v.act_a[a, 8 * b : 8 * b + N, 0:channels]
                k = (3 * a + b) * channels
                term = dot(act, weight[k : k + channels, 0:C])
                total = term if total is None else total + term
        return total

    stats = reduce_end(0, 2 * C)
    halo_wait(0, v.jx)
    activate(v.jx, stats, v.gain_one[...].reshape(1, 2 * C))

    owners = [(lax.rem(r + i, R)) for i in range(1, R)]
    for owner in owners:
        f_over(owner, 1 - xx).wait_recv()
        f_mate_extra(owner).start()
    mate_rows = v.fp.at[pl.ds(0, R - 1), pl.ds(0, share * UNIT)]
    all_of(mate_rows, 10).wait_recv()
    for owner in range(R):
        unpack(v.fp[owner], v.fw, owner * fk)

    hidden_one = conv(2 * C, v.fw) + time_shift
    keep_own(v.hx, hidden_one)
    reduce_start(1, jnp.sum(hidden_one, axis=0, keepdims=True),
                 jnp.sum(hidden_one * hidden_one, axis=0, keepdims=True))
    halo_send(1, v.hx)

    mid_twin_in.wait_recv()
    mid_mate[2].start()
    for copy in mid_mate_in:
        copy.wait_recv()
    for owner in range(Q):
        unpack(v.mp[owner], v.mw, owner * mk)
    shortcut = dot(rows_of(v.jx, 2 * C, 8, N).astype(BF16), v.sw[...])
    stats = reduce_end(1, C)
    halo_wait(1, v.hx)
    activate(v.hx, stats, v.gain_two[...].reshape(1, C))
    block_out = conv(C, v.mw) + shortcut

    keep_own(v.ox, block_out)
    reduce_start(2, jnp.sum(block_out, axis=0, keepdims=True),
                 jnp.sum(block_out * block_out, axis=0, keepdims=True))
    halo_send(2, v.ox)
    stats = reduce_end(2, C)
    halo_wait(2, v.ox)

    center, inverse = stats
    z = silu((rows_of(v.ox, C, 0, N + 16) - center) * (inverse * v.gain_three[...].reshape(1, C)))
    z = jnp.where(inside, z.reshape(W + 2, 8, C), 0.0).reshape(N + 16, C)
    spread = dot(z.astype(BF16), out_taps)
    lane = lax.broadcasted_iota(jnp.int32, (N, LANES), 1)
    row = lax.broadcasted_iota(jnp.int32, (W, 8, 1), 1)
    total = None
    for a in range(3):
        got = None
        for b in range(3):
            t = couts * (3 * a + b)
            here = jnp.where(
                (lane >= t) & (lane < t + couts), spread[8 * b : 8 * b + N, :], 0.0)
            got = here if got is None else got + here
        got = got.reshape(W, 8, LANES)
        if a == 0:
            got = jnp.where(row > 0, pltpu.roll(got, 1, 1), 0.0)
        elif a == 2:
            got = jnp.where(row < 7, pltpu.roll(got, 7, 1), 0.0)
        total = got if total is None else total + got
    v.tap[...] = total.reshape(N, LANES)
    ordered = jnp.concatenate([v.tap[pl.ds(q, W, 8), :] for q in range(R)], axis=0)
    fold = (lax.rem(lax.broadcasted_iota(jnp.int32, (8, LANES), 1), couts)
            == lax.broadcasted_iota(jnp.int32, (8, LANES), 0)).astype(F32)
    rows = dot_nt(fold, ordered, lax.Precision.HIGHEST)[0:couts]
    for q in range(R):
        v.outs[q, :, 0:W] = rows[:, W * q : W * (q + 1)]

    def out_copy(q, rr):
        return remote(v.outs.at[q], v.outr.at[s], v.one_s.at[4], v.one_r.at[4], rr, c)

    for q in range(R):
        @pl.when(r != q)
        def _():
            out_copy(q, q).start()

        @pl.when(r == q)
        def _():
            v.outr[s] = v.outs[q]

    all_of(v.outr.at[pl.ds(0, R - 1)], 4).wait_recv()
    for q in range(R):
        noise[:, W * q : W * (q + 1)] = v.outr[q, :, 0:W]

    all_of(v.lat.at[0, pl.ds(0, R - 1)], 0).wait_send()

    @pl.when(c > 0)
    def _():
        lat_left().wait_send()

    @pl.when(c < Q - 1)
    def _():
        lat_right().wait_send()

    all_of(v.a2a.at[pl.ds(0, R - 1)], 3).wait_send()
    all_of(v.outr.at[pl.ds(0, R - 1)], 4).wait_send()
    all_of(v.emb.at[pl.ds(0, Q - 1)], 5).wait_send()
    for stage, ext in enumerate((v.jx, v.hx, v.ox)):
        sum_all(stage).wait_send()

        @pl.when(has_left)
        def _():
            halo_left(stage, ext).wait_send()

        @pl.when(has_right)
        def _():
            halo_right(stage, ext).wait_send()
    for copy in mid_over + (mid_twin,) + mid_mate:
        copy.wait_send()
    moved = (share - ALONE) * UNIT
    level = r // 2
    for count in range(1, R // 2):
        @pl.when(level == count - 1)
        def _():
            all_of(v.fp.at[pl.ds(0, count), pl.ds(0, moved)], 6).wait_send()

        @pl.when(level == R // 2 - count)
        def _():
            all_of(v.fp.at[pl.ds(0, count), pl.ds(0, moved)], 7).wait_send()

    all_of(v.fp.at[pl.ds(0, R // 2), pl.ds(0, moved)], 8).wait_send()
    all_of(v.fp.at[pl.ds(0, R - 1), pl.ds(0, ALONE * UNIT)], 9).wait_send()
    all_of(mate_rows, 10).wait_send()


def fast_shards(
    R, Q,
    latent, deep, timestep, in_weight, front_weight, middle_weight, skip_weight, out_weight,
    time_weight, time_second, time_proj, input_gain, middle_gain, output_gain,
):
    C = deep.shape[0]
    cin = latent.shape[0]
    px = deep.shape[1] * deep.shape[2]
    couts = out_weight.shape[1]
    W = px // R
    N = W * 8
    CP = (C + LANES - 1) // LANES * LANES
    fk, mk, skr = front_weight.shape[0], middle_weight.shape[0], skip_weight.shape[0]
    hbm = pl.BlockSpec(memory_space=pl.ANY)
    vmem = pl.BlockSpec(memory_space=pltpu.VMEM)
    smem = pl.BlockSpec(memory_space=pltpu.SMEM)
    dma = pltpu.SemaphoreType.DMA
    args = (
        latent.reshape(cin, px), deep.reshape(C, px), timestep, in_weight, front_weight.T,
        middle_weight.T, skip_weight, out_weight.T, time_weight, time_second, time_proj.T,
        input_gain, middle_gain, output_gain,
    )
    fq, wide = time_weight.shape
    shapes = dict(
        lat_v=pltpu.VMEM((cin, px), BF16), lat=pltpu.VMEM((3, R, cin, px), BF16),
        latrows=pltpu.VMEM((3, R * cin, px), F32), deep_v=pltpu.VMEM((C, px), BF16),
        dr=pltpu.VMEM((px, CP), BF16), a2a=pltpu.VMEM((R, W, CP), BF16),
        inw=pltpu.VMEM((9 * cin, C), BF16), wb=pltpu.VMEM((3, R * cin, R * CP), F32),
        sk=pltpu.VMEM((W, R * CP), F32), jx=pltpu.VMEM((2 * C // LANES, N + 16, LANES), F32),
        hx=pltpu.VMEM((CP // LANES, N + 16, LANES), F32),
        ox=pltpu.VMEM((CP // LANES, N + 16, LANES), F32),
        act_a=pltpu.VMEM((3, N + 16, 2 * C), BF16), act_b=pltpu.VMEM((3, N, 2 * C), BF16),
        front_v=pltpu.VMEM((C, fk), BF16), fw=pltpu.VMEM((18 * C, CP), BF16),
        fp=pltpu.VMEM((R, PACK * UNIT, 2 * C), BF16), mp=pltpu.VMEM((Q, PACK * UNIT, 2 * C), BF16),
        mid_v=pltpu.VMEM((C, mk), BF16), mw=pltpu.VMEM((9 * C, CP), BF16),
        sw=pltpu.VMEM((2 * C, C), BF16), outw_v=pltpu.VMEM((couts, 9 * C), BF16),
        wr32=pltpu.VMEM((LANES, C), F32), tw=pltpu.VMEM((fq, wide), BF16),
        ts=pltpu.VMEM(time_second.shape, BF16), tp=pltpu.VMEM((C, wide), BF16),
        part=pltpu.VMEM((1, fq), F32), emb=pltpu.VMEM((Q, 1, wide), F32),
        sums=pltpu.VMEM((3, R * Q, 1, LANES), F32), tap=pltpu.VMEM((N, LANES), F32),
        outs=pltpu.VMEM((R, couts, LANES), F32), outr=pltpu.VMEM((R, couts, LANES), F32),
        gain_one=pltpu.VMEM((2 * C,), F32), gain_two=pltpu.VMEM((C,), F32),
        gain_three=pltpu.VMEM((C,), F32),
        ld_s=dma((13,)), one_s=dma((11,)), one_r=dma((11,)), halo_s=dma((3, 2)), halo_r=dma((3, 2)),
        fm_r=dma((2, R)), fx_r=dma((R,)), mid_s=dma((7,)), mid_r=dma((7,)),
        sum_s=dma((3,)), sum_r=dma((3,)),
    )
    specs = [hbm] * len(args)
    specs[2] = smem
    out = pl.pallas_call(
        functools.partial(fast_kernel, R, Q, tuple(shapes)),
        out_shape=jax.ShapeDtypeStruct((couts, px), F32),
        in_specs=specs,
        out_specs=vmem,
        scratch_shapes=list(shapes.values()),
        compiler_params=pltpu.CompilerParams(
            collective_id=0, has_side_effects=True, vmem_limit_bytes=56 * 1024 * 1024
        ),
    )(*args)
    return out.reshape(couts, 1, px)


def solution(mesh):
    R, Q = mesh.shape["rows"], mesh.shape["cols"]

    def body(*args):
        deep, front = args[1], args[4]
        fits = (
            R == 8 and Q == 4 and deep.shape[1] == 1 and deep.shape[2] % (R * LANES // 4) == 0
            and front.shape[0] % UNIT == 0
            and PACK * UNIT < front.shape[0] <= 2 * PACK * UNIT
            and args[5].shape[0] == front.shape[0] and deep.shape[0] % LANES * 2 == LANES)
        return (fast_shards if fits else shards)(R, Q, *args)

    return jax.shard_map(
        body,
        mesh=mesh,
        in_specs=(
            P(None, "rows", "cols"), P(None, "rows", "cols"), P(), P(),
            P("rows", None), P("cols", None), P("cols", None), P(),
            P(), P("cols", None), P(), P(), P(), P(),
        ),
        out_specs=P(None, "rows", "cols"),
        check_vma=False,
    )
```

profile of v0, /device:TPU:0, one launch (start us, length us, event | category | flops | bytes accessed | tf_op | source)
XLA Modules:
  0.0 55.0 jit_solution(4500686808405418173)
XLA Ops:
  0.7 53.1 %shard_map.136 = f32[4,256]{1,0:T(4,128)} custom-call(bf16[4,256]{1,0:T(4,128)(2,1)} %bitcast.13, bf16[320,256]{1,0:T(8,128)(2,1)} %bitcast.10, s32[1]{0:T(128)S(6)} %copy.16.timestep, bf16[36,320]{1,0:T(8,128)(2,1)} %in_w.1, bf16[320,720]{1,0:T(8,128)(2,1)} %bitcast.8, bf16[320,720]{1,0:T(8,128)(2,1)} %bitcast.9, bf16[160,320]{1,0:T(8,128)(2,1)} %skip.1, ...), custom_call_target="tpu_custom_call" | custom-call | tf_op jit(solution)/shard_map/pallas_call | solution.py:1122
  53.7 1.3 %copy.15 = f32[4,1,256]{2,1,0:T(1,128)} copy(f32[4,1,256]{2,0,1:T(4,128)} %bitcast.12) | data formatting | bytes 8192 | tf_op jit(solution)/shard_map/reshape | solution.py:1132
where the time goes:
time: 55.2 us; the launch traced here: 55 us
  Pallas kernels  53.1 us (96%)
  local copies, waits for them, and re-layouts  1.28 us (2%)
  between operations  0.66 us (1%)
    pallas_call x1, Pallas kernels, fast_shards(): pl.pallas_call(functools.partial(fast_kernel, R, Q, tuple(shapes)), out_s...  53.1 us
    reshape x1, local copies, waits for them, and re-layouts, fast_shards(): return out.reshape(couts, 1, px)  1.28 us

commit v1 on v0

--- a/solution.py
+++ b/solution.py
@@ -521,7 +521,7 @@
     mk, skr, fk = middle.shape[1], skip.shape[0], front.shape[1]
     loads = {}
     for k, (name, src, dst) in enumerate((
-        ("deep", deep, v.deep_v), ("front", front, v.front_v), ("latent", latent, v.lat_v),
+        ("front", front, v.front_v), ("latent", latent, v.lat_v), ("deep", deep, v.deep_v),
         ("in", in_w, v.inw), ("tw", time_w, v.tw), ("ts", time_s, v.ts),
         ("middle", middle, v.mid_v),
         ("skip", skip, v.sw.at[pl.ds(pl.multiple_of(c * skr, TILE), skr)]),
@@ -532,13 +532,6 @@
         loads[name] = pltpu.make_async_copy(src, dst, v.ld_s.at[k])
         loads[name].start()
 
-    loads["deep"].wait()
-    deep_t = v.deep_v[...].astype(F32).T
-    v.dr[:, C:CP] = jnp.zeros((px, GAP), BF16)
-    v.dr[:, 0:C] = deep_t.astype(BF16)
-    pad = jnp.zeros((1, GAP), F32)
-    deep_top = jnp.concatenate([jnp.sum(deep_t, axis=0, keepdims=True), pad], axis=1)
-    deep_low = jnp.concatenate([jnp.sum(deep_t * deep_t, axis=0, keepdims=True), pad], axis=1)
     tall = PACK * UNIT
     main = C // LANES * LANES
     tail = C - main
@@ -593,13 +586,10 @@
     y = lax.rem(r, 2)
     twin = r + 1 - 2 * y
     share = PACK // 2
-    both = (share - 2 * ALONE) // 2
-    sizes = {0: ALONE + both, 1: both, "E": ALONE}
+    sizes = (ALONE, share - 2 * ALONE)
 
     def f_part(owner, part, x_of, core_of):
-        first = {
-            0: x_of * (ALONE + both), 1: ALONE + both - x_of * both, "E": x_of * (ALONE + 2 * both),
-        }[part]
+        first = (x_of * (share - ALONE), ALONE)[part]
         return v.fp.at[owner, pl.ds(
             pl.multiple_of((core_of * share + first) * UNIT, UNIT), sizes[part] * UNIT)]
 
@@ -617,7 +607,7 @@
         return f_move(owner, part, v.one_s.at[8], twin, c)
 
     def f_over(owner, x_of):
-        ref = f_part(owner, "E", x_of, core)
+        ref = f_part(owner, 0, x_of, core)
         return remote(ref, ref, v.one_s.at[9], v.fx_r.at[owner], r, over)
 
     def f_mate(owner, part):
@@ -625,7 +615,7 @@
         return remote(ref, ref, v.one_s.at[10], v.one_r.at[10], r, mate)
 
     def f_mate_extra(owner):
-        ref = f_part(owner, "E", 1 - xx, core)
+        ref = f_part(owner, 0, 1 - xx, core)
         return remote(ref, ref, v.one_s.at[10], v.one_r.at[10], r, mate)
 
     def when_row(t, body):
@@ -659,6 +649,15 @@
             f_over(owner, xx).start()
         f_mate(owner, part).start()
 
+    def from_x(owner):
+        f_over(owner, 1 - xx).wait_recv()
+        f_mate_extra(owner).start()
+
+    def x_steps(d, twins):
+        for sign in (-1, 1):
+            t = r + sign * 2 * d
+            when_row(t, lambda: from_x(t + twins * (twin - r)))
+
     def z_steps(d):
         for part in (0, 1):
             for sign in (-1, 1):
@@ -670,44 +669,60 @@
                 t = r + sign * 2 * d
                 when_row(t, lambda: from_y(t + twin - r, part))
 
+    loads["middle"].wait()
+    v.mp[c] = packed(v.mid_v, mk)
+    loads["skip"].wait()
+    quarter = tall // 4
+
+    def mid_copy(ref, n, rr, cc):
+        return remote(ref, ref, v.mid_s.at[n], v.mid_r.at[n], rr, cc)
+
+    def mid_rows(owner, n, of):
+        return v.mp.at[owner, pl.ds(pl.multiple_of((2 * of + n) * quarter, UNIT), quarter)]
+
+    def skip_rows(owner):
+        return v.sw.at[pl.ds(pl.multiple_of(owner * skr, TILE), skr)]
+
+    far = lax.rem(mate + 2, Q)
+
+    def mid_over(n, owner):
+        ref = skip_rows(owner) if n == 2 else mid_rows(owner, n, y)
+        return mid_copy(ref, n, r, over)
+
+    def mid_twin(n, of):
+        return mid_copy(mid_rows(over, n, of), 3 + n, twin, c)
+
+    def mid_on(n, owner, of):
+        ref = skip_rows(owner) if n == 4 else mid_rows(owner, n % 2, of)
+        return mid_copy(ref, 5 + n, r, mate)
+
+    def mid_mate(owner):
+        return (mid_copy(v.mp.at[owner], 10, r, mate), mid_copy(skip_rows(owner), 11, r, mate))
+
+    mid_over(0, c).start()
+    for copy in mid_mate(c):
+        copy.start()
+
+    loads["deep"].wait()
+    deep_t = v.deep_v[...].astype(F32).T
+    v.dr[:, C:CP] = jnp.zeros((px, GAP), BF16)
+    v.dr[:, 0:C] = deep_t.astype(BF16)
+    pad = jnp.zeros((1, GAP), F32)
+    deep_top = jnp.concatenate([jnp.sum(deep_t, axis=0, keepdims=True), pad], axis=1)
+    deep_low = jnp.concatenate([jnp.sum(deep_t * deep_t, axis=0, keepdims=True), pad], axis=1)
     def a2a_copy(q):
         return remote(v.dr.at[pl.ds(W * q, W)], v.a2a.at[r], v.one_s.at[3], v.one_r.at[3],
                       snake(q, c, R), c)
 
-    for q in range(R):
-        @pl.when(s != q)
-        def _():
-            a2a_copy(q).start()
-
-        @pl.when(s == q)
-        def _():
-            v.a2a[r] = v.dr[pl.ds(W * q, W), :]
-
-    loads["middle"].wait()
-    v.mp[c] = packed(v.mid_v, mk)
-    loads["skip"].wait()
-    cut_rows = tall // 2
-
-    def mid_half(owner, which):
-        return v.mp.at[owner, pl.ds(pl.multiple_of(which * cut_rows, UNIT), cut_rows)]
-
-    def skip_rows(owner):
-        return v.sw.at[pl.ds(pl.multiple_of(owner * skr, TILE), skr)]
-
-    def mid_copy(ref, n, rr, cc):
-        return remote(ref, ref, v.mid_s.at[n], v.mid_r.at[n], rr, cc)
-
-    mid_over = (mid_copy(mid_half(c, y), 0, r, over), mid_copy(skip_rows(c), 1, r, over))
-    mid_over_in = (mid_copy(mid_half(over, y), 0, r, over), mid_copy(skip_rows(over), 1, r, over))
-    mid_twin = mid_copy(mid_half(over, y), 2, twin, c)
-    mid_twin_in = mid_copy(mid_half(over, 1 - y), 2, twin, c)
-    mid_mate = (mid_copy(v.mp.at[c], 3, r, mate), mid_copy(skip_rows(c), 4, r, mate),
-                mid_copy(v.mp.at[over], 5, r, mate), mid_copy(skip_rows(over), 6, r, mate))
-    far = lax.rem(mate + 2, Q)
-    mid_mate_in = (mid_copy(v.mp.at[mate], 3, r, mate), mid_copy(skip_rows(mate), 4, r, mate),
-                   mid_copy(v.mp.at[far], 5, r, mate), mid_copy(skip_rows(far), 6, r, mate))
-    for copy in mid_over + mid_mate[0:2]:
-        copy.start()
+    def a2a_send():
+        for q in range(R):
+            @pl.when(s != q)
+            def _():
+                a2a_copy(q).start()
+
+            @pl.when(s == q)
+            def _():
+                v.a2a[r] = v.dr[pl.ds(W * q, W), :]
 
     loads["in"].wait()
     inw = v.inw[...].astype(F32)
@@ -794,7 +809,7 @@
         size = channels // GROUPS
         ch = lax.broadcasted_iota(jnp.int32, shape, 1 if flip else 0)
         g = lax.broadcasted_iota(jnp.int32, shape, 0 if flip else 1)
-        return ((ch >= g * size) & (ch < g * size + size)).astype(F32)
+        return ((ch >= g * size) & (ch < g * size + size)).astype(F32).astype(BF16)
 
     def sum_copy(stage, slot, i, rr, cc):
         return remote(v.sums.at[stage, slot], v.sums.at[stage, slot],
@@ -802,9 +817,10 @@
 
     def reduce_start(stage, top, low):
         channels = top.shape[1]
-        both = jnp.concatenate([top, low, jnp.zeros((6, channels), F32)], axis=0)
-        res = dot(both, indicator(channels, False), lax.Precision.HIGHEST)
-        v.sums[stage, me] = res[0:1] + pltpu.roll(res, GROUPS, 1)[1:2]
+        res = dot(jnp.concatenate([pieces_of(top), pieces_of(low)], axis=0),
+                  indicator(channels, False))
+        v.sums[stage, me] = jnp.sum(res[0:3], axis=0, keepdims=True) + pltpu.roll(
+            jnp.sum(res[3:6], axis=0, keepdims=True), GROUPS, 1)
         for n, (i, j) in enumerate(others):
             sum_copy(stage, me, n, lax.rem(r + i, R), lax.rem(c + j, Q)).start()
 
@@ -817,10 +833,12 @@
         total = jnp.sum(v.sums[stage], axis=0) / (channels // GROUPS * image)
         spread = pltpu.roll(total, LANES - GROUPS, 1) - total * total
         inverse = lax.rsqrt(jnp.maximum(spread, 0.0) + EPS)
-        both = jnp.concatenate([total, inverse, jnp.zeros((6, LANES), F32)], axis=0)
-        both = jnp.where(lax.broadcasted_iota(jnp.int32, (8, LANES), 1) < GROUPS, both, 0.0)
-        wide = dot(both, indicator(channels, True), lax.Precision.HIGHEST)
-        return wide[0:1], wide[1:2]
+        group = lax.broadcasted_iota(jnp.int32, (1, LANES), 1) < GROUPS
+        wide = dot(jnp.concatenate([pieces_of(jnp.where(group, row, 0.0))
+                                    for row in (total, inverse)], axis=0),
+                   indicator(channels, True))
+        return (jnp.sum(wide[0:3], axis=0, keepdims=True),
+                jnp.sum(wide[3:6], axis=0, keepdims=True))
 
     reduce_start(0, join(deep_top, skip_top), join(deep_low, skip_low))
 
@@ -869,23 +887,29 @@
     z_steps(1)
     for part in (0, 1):
         from_y(twin, part)
-
+    z_steps(2)
+    a2a_send()
+    mid_over(1, c).start()
+    y_steps(1)
+    for d in range(3, R // 2):
+        z_steps(d)
+        y_steps(d - 1)
     all_of(v.a2a.at[pl.ds(0, R - 1)], 3).wait_recv()
     for q in range(R):
         joined = join(v.a2a[q].astype(F32), v.sk[:, q * CP : (q + 1) * CP])
         for n in range(2 * C // LANES):
             v.jx[n, pl.ds(8 + q, W, 8), :] = joined[:, n * LANES : (n + 1) * LANES]
     halo_send(0, v.jx)
-    z_steps(2)
-    y_steps(1)
-    for d in range(3, R // 2):
-        z_steps(d)
-        y_steps(d - 1)
+    from_x(twin)
+    x_steps(1, 0)
+    x_steps(2, 0)
+    x_steps(1, 1)
     y_steps(R // 2 - 1)
-    for copy in mid_over_in:
-        copy.wait_recv()
-    for copy in (mid_twin, mid_mate[3]):
-        copy.start()
+    mid_over(2, c).start()
+    for n in (0, 1):
+        mid_over(n, over).wait_recv()
+        mid_twin(n, y).start()
+        mid_on(n, over, y).start()
 
     loads["out"].wait()
     loads["tp"].wait()
@@ -947,14 +971,14 @@
                 total = term if total is None else total + term
         return total
 
+    for d in range(3, R // 2):
+        x_steps(d, 0)
+        x_steps(d - 1, 1)
+    x_steps(R // 2 - 1, 1)
     stats = reduce_end(0, 2 * C)
     halo_wait(0, v.jx)
     activate(v.jx, stats, v.gain_one[...].reshape(1, 2 * C))
 
-    owners = [(lax.rem(r + i, R)) for i in range(1, R)]
-    for owner in owners:
-        f_over(owner, 1 - xx).wait_recv()
-        f_mate_extra(owner).start()
     mate_rows = v.fp.at[pl.ds(0, R - 1), pl.ds(0, share * UNIT)]
     all_of(mate_rows, 10).wait_recv()
     for owner in range(R):
@@ -966,10 +990,15 @@
                  jnp.sum(hidden_one * hidden_one, axis=0, keepdims=True))
     halo_send(1, v.hx)
 
-    mid_twin_in.wait_recv()
-    mid_mate[2].start()
-    for copy in mid_mate_in:
+    mid_over(2, over).wait_recv()
+    mid_on(4, over, y).start()
+    for n in (0, 1):
+        mid_twin(n, 1 - y).wait_recv()
+        mid_on(2 + n, over, 1 - y).start()
+    for copy in mid_mate(mate):
         copy.wait_recv()
+    for n in range(5):
+        mid_on(n, far, y if n < 2 else 1 - y).wait_recv()
     for owner in range(Q):
         unpack(v.mp[owner], v.mw, owner * mk)
     shortcut = dot(rows_of(v.jx, 2 * C, 8, N).astype(BF16), v.sw[...])
@@ -1052,7 +1081,13 @@
         @pl.when(has_right)
         def _():
             halo_right(stage, ext).wait_send()
-    for copy in mid_over + (mid_twin,) + mid_mate:
+    for n in range(3):
+        mid_over(n, c).wait_send()
+    for n in range(2):
+        mid_twin(n, y).wait_send()
+    for n in range(5):
+        mid_on(n, over, y if n < 2 else 1 - y).wait_send()
+    for copy in mid_mate(c):
         copy.wait_send()
     moved = (share - ALONE) * UNIT
     level = r // 2
@@ -1114,7 +1149,7 @@
         gain_one=pltpu.VMEM((2 * C,), F32), gain_two=pltpu.VMEM((C,), F32),
         gain_three=pltpu.VMEM((C,), F32),
         ld_s=dma((13,)), one_s=dma((11,)), one_r=dma((11,)), halo_s=dma((3, 2)), halo_r=dma((3, 2)),
-        fm_r=dma((2, R)), fx_r=dma((R,)), mid_s=dma((7,)), mid_r=dma((7,)),
+        fm_r=dma((2, R)), fx_r=dma((R,)), mid_s=dma((12,)), mid_r=dma((12,)),
         sum_s=dma((3,)), sum_r=dma((3,)),
     )
     specs = [hbm] * len(args)

time: 55.2 us -> 51.9 us (0.940)
  Pallas kernels: 53.1 us -> 49.7 us
    pallas_call x1, Pallas kernels: 53.1 us -> 49.7 us  [fast_shards(): pl.pallas_call(functools.partial(fast_kernel, R, Q, tuple(shapes)), out_s...]
where the time goes in v1:
time: 51.9 us; the launch traced here: 51.7 us
  Pallas kernels  49.7 us (96%)
  local copies, waits for them, and re-layouts  1.28 us (2%)
  between operations  0.66 us (1%)
    pallas_call x1, Pallas kernels, fast_shards(): pl.pallas_call(functools.partial(fast_kernel, R, Q, tuple(shapes)), out_s...  49.7 us
    reshape x1, local copies, waits for them, and re-layouts, fast_shards(): return out.reshape(couts, 1, px)  1.28 us

profile of v1, /device:TPU:0, one launch (start us, length us, event | category | flops | bytes accessed | tf_op | source)
XLA Modules:
  0.0 51.7 jit_solution(3394370816900440867)
XLA Ops:
  0.7 49.7 %shard_map.136 = f32[4,256]{1,0:T(4,128)} custom-call(bf16[4,256]{1,0:T(4,128)(2,1)} %bitcast.13, bf16[320,256]{1,0:T(8,128)(2,1)} %bitcast.10, s32[1]{0:T(128)S(6)} %copy.16.timestep, bf16[36,320]{1,0:T(8,128)(2,1)} %in_w.1, bf16[320,720]{1,0:T(8,128)(2,1)} %bitcast.8, bf16[320,720]{1,0:T(8,128)(2,1)} %bitcast.9, bf16[160,320]{1,0:T(8,128)(2,1)} %skip.1, ...), custom_call_target="tpu_custom_call" | custom-call | tf_op jit(solution)/shard_map/pallas_call | solution.py:1157
  50.4 1.3 %copy.15 = f32[4,1,256]{2,1,0:T(1,128)} copy(f32[4,1,256]{2,0,1:T(4,128)} %bitcast.12) | data formatting | bytes 8192 | tf_op jit(solution)/shard_map/reshape | solution.py:1167

commit v2 on v1

--- a/solution.py
+++ b/solution.py
@@ -511,11 +511,18 @@
             device_id={"rows": rr, "cols": cc}, device_id_type=MESH,
         )
 
-    others = [(i, j) for i in range(R) for j in range(Q) if (i, j) != (0, 0)]
+    def flipped(value, mask, bits):
+        for b in range(bits):
+            if mask >> b & 1:
+                value = value + (1 - 2 * lax.rem(value // (1 << b), 2)) * (1 << b)
+        return value
+
+    others = [(flipped(r, i, 3), flipped(c, j, 2))
+              for i in reversed(range(R)) for j in reversed(range(Q)) if (i, j) != (0, 0)]
     barrier = pltpu.get_barrier_semaphore()
     for i, j in others:
         pl.semaphore_signal(
-            barrier, inc=1, device_id={"rows": lax.rem(r + i, R), "cols": lax.rem(c + j, Q)},
+            barrier, inc=1, device_id={"rows": i, "cols": j},
             device_id_type=MESH)
 
     mk, skr, fk = middle.shape[1], skip.shape[0], front.shape[1]
@@ -543,13 +550,16 @@
         return jnp.concatenate([first[:, 0:main], mixed, second[:, 0:main]], axis=1).astype(BF16)
 
     def unpack(block, ref, start):
+        def at(first):
+            return pl.ds(first if isinstance(first, int) else pl.multiple_of(first, UNIT), tall)
+
         mixed = block[:, main : main + LANES]
-        ref[start : start + tall, 0:main] = block[:, 0:main]
-        ref[start : start + tall, main : main + LANES] = mixed
+        ref[at(start), 0:main] = block[:, 0:main]
+        ref[at(start), main : main + LANES] = mixed
         swapped = pltpu.roll(mixed.astype(F32), LANES - tail, 1).astype(BF16)
         start = start + fk - tall
-        ref[start : start + tall, 0:main] = block[:, main + LANES : 2 * C]
-        ref[start : start + tall, main : main + LANES] = swapped
+        ref[at(start), 0:main] = block[:, main + LANES : 2 * C]
+        ref[at(start), main : main + LANES] = swapped
 
     loads["latent"].wait()
     v.lat[0, r] = v.lat_v[...]
@@ -612,11 +622,11 @@
 
     def f_mate(owner, part):
         ref = f_part(owner, part, xx, core)
-        return remote(ref, ref, v.one_s.at[10], v.one_r.at[10], r, mate)
+        return remote(ref, ref, v.one_s.at[10], v.fo_r.at[owner], r, mate)
 
     def f_mate_extra(owner):
         ref = f_part(owner, 0, 1 - xx, core)
-        return remote(ref, ref, v.one_s.at[10], v.one_r.at[10], r, mate)
+        return remote(ref, ref, v.one_s.at[10], v.fo_r.at[owner], r, mate)
 
     def when_row(t, body):
         @pl.when((t >= 0) & (t < R))
@@ -675,7 +685,8 @@
     quarter = tall // 4
 
     def mid_copy(ref, n, rr, cc):
-        return remote(ref, ref, v.mid_s.at[n], v.mid_r.at[n], rr, cc)
+        kind = 1 if n in (2, 9, 11) else 0
+        return remote(ref, ref, v.mid_s.at[kind], v.mid_r.at[n], rr, cc)
 
     def mid_rows(owner, n, of):
         return v.mp.at[owner, pl.ds(pl.multiple_of((2 * of + n) * quarter, UNIT), quarter)]
@@ -723,6 +734,8 @@
             @pl.when(s == q)
             def _():
                 v.a2a[r] = v.dr[pl.ds(W * q, W), :]
+
+    unpack(v.fp[r], v.fw, r * fk)
 
     loads["in"].wait()
     inw = v.inw[...].astype(F32)
@@ -822,7 +835,7 @@
         v.sums[stage, me] = jnp.sum(res[0:3], axis=0, keepdims=True) + pltpu.roll(
             jnp.sum(res[3:6], axis=0, keepdims=True), GROUPS, 1)
         for n, (i, j) in enumerate(others):
-            sum_copy(stage, me, n, lax.rem(r + i, R), lax.rem(c + j, Q)).start()
+            sum_copy(stage, me, n, i, j).start()
 
     def sum_all(stage):
         ref = v.sums.at[stage, pl.ds(0, R * Q - 1)]
@@ -958,33 +971,76 @@
                 v.act_a[a, :, lo:hi] = flat.astype(BF16)
                 v.act_b[a, :, lo:hi] = flat[8 : N + 8].astype(BF16)
 
-    def conv(channels, weight):
+    def conv_whole(channels, weight):
+        acts = [v.act_b[a] if b == 1 else v.act_a[a, 8 * b : 8 * b + N]
+                for a in range(3) for b in range(3)]
+        return dot(jnp.concatenate(acts, axis=1), weight[:, 0:C])
+
+    def activate_wide(ext, stats, gain):
+        center, inverse = stats
+        z = silu((rows_of(ext, C, 0, N + 16) - center) * (inverse * gain))
+        z = jnp.where(inside, z.reshape(W + 2, 8, C), 0.0)
+        moved = (jnp.where(row > 0, pltpu.roll(z, 1, 1), 0.0), z,
+                 jnp.where(row < 7, pltpu.roll(z, 7, 1), 0.0))
+        wide = jnp.concatenate([m.reshape(N + 16, C) for m in moved], axis=1)
+        v.act_c[...] = wide.astype(BF16)
+        v.act_d[...] = wide[8 : N + 8].astype(BF16)
+
+    def conv_columns(weight):
         total = None
-        for a in range(3):
-            for b in range(3):
-                if b == 1:
-                    act = v.act_b[a, :, 0:channels]
+        for b, act in enumerate((v.act_c[0:N], v.act_d[...], v.act_c[16 : N + 16])):
+            term = dot(act, weight[3 * C * b : 3 * C * (b + 1), 0:C])
+            total = term if total is None else total + term
+        return total
+
+    def unpack_columns(owner):
+        for side in (0, 1):
+            first = owner * mk + side * tall
+            stop = owner * mk + (tall if side == 0 else mk)
+            while first < stop:
+                tap, inside_tap = divmod(first, C)
+                count = min(C - inside_tap, stop - first)
+                at = first - owner * mk - side * (mk - tall)
+                to = (tap % 3 * 3 + tap // 3) * C + inside_tap
+                block = v.mp[owner, at : at + count]
+                mixed = block[:, main : main + LANES]
+                if side == 0:
+                    v.mw[to : to + count, 0:main] = block[:, 0:main]
                 else:
-                    act = v.act_a[a, 8 * b : 8 * b + N, 0:channels]
-                k = (3 * a + b) * channels
-                term = dot(act, weight[k : k + channels, 0:C])
-                total = term if total is None else total + term
-        return total
+                    v.mw[to : to + count, 0:main] = block[:, main + LANES : 2 * C]
+                    mixed = pltpu.roll(mixed.astype(F32), LANES - tail, 1).astype(BF16)
+                v.mw[to : to + count, main : main + LANES] = mixed
+                first += count
 
     for d in range(3, R // 2):
         x_steps(d, 0)
         x_steps(d - 1, 1)
     x_steps(R // 2 - 1, 1)
+
+    def ready(owner):
+        ref = v.fp.at[owner, pl.ds(0, share * UNIT)]
+        remote(ref, ref, v.one_s.at[10], v.fo_r.at[owner], r, mate).wait_recv()
+        unpack(v.fp[owner], v.fw, owner * fk)
+
+    def when_pair(d, twins, body):
+        for sign in (-1, 1):
+            t = r + sign * 2 * d
+            when_row(t, lambda: body(t + twins * (twin - r)))
+
+    ready(twin)
+    when_pair(1, 0, ready)
+    when_pair(1, 1, ready)
+    for d in range(2, R // 2 - 1):
+        when_pair(d, 0, ready)
     stats = reduce_end(0, 2 * C)
     halo_wait(0, v.jx)
     activate(v.jx, stats, v.gain_one[...].reshape(1, 2 * C))
 
-    mate_rows = v.fp.at[pl.ds(0, R - 1), pl.ds(0, share * UNIT)]
-    all_of(mate_rows, 10).wait_recv()
-    for owner in range(R):
-        unpack(v.fp[owner], v.fw, owner * fk)
-
-    hidden_one = conv(2 * C, v.fw) + time_shift
+    for d in range(2, R // 2):
+        when_pair(d, 1, ready)
+    when_pair(R // 2 - 1, 0, ready)
+
+    hidden_one = conv_whole(2 * C, v.fw) + time_shift
     keep_own(v.hx, hidden_one)
     reduce_start(1, jnp.sum(hidden_one, axis=0, keepdims=True),
                  jnp.sum(hidden_one * hidden_one, axis=0, keepdims=True))
@@ -1000,12 +1056,12 @@
     for n in range(5):
         mid_on(n, far, y if n < 2 else 1 - y).wait_recv()
     for owner in range(Q):
-        unpack(v.mp[owner], v.mw, owner * mk)
+        unpack_columns(owner)
     shortcut = dot(rows_of(v.jx, 2 * C, 8, N).astype(BF16), v.sw[...])
     stats = reduce_end(1, C)
     halo_wait(1, v.hx)
-    activate(v.hx, stats, v.gain_two[...].reshape(1, C))
-    block_out = conv(C, v.mw) + shortcut
+    activate_wide(v.hx, stats, v.gain_two[...].reshape(1, C))
+    block_out = conv_columns(v.mw) + shortcut
 
     keep_own(v.ox, block_out)
     reduce_start(2, jnp.sum(block_out, axis=0, keepdims=True),
@@ -1081,14 +1137,8 @@
         @pl.when(has_right)
         def _():
             halo_right(stage, ext).wait_send()
-    for n in range(3):
-        mid_over(n, c).wait_send()
-    for n in range(2):
-        mid_twin(n, y).wait_send()
-    for n in range(5):
-        mid_on(n, over, y if n < 2 else 1 - y).wait_send()
-    for copy in mid_mate(c):
-        copy.wait_send()
+    for kind, ref in enumerate((v.mp.at[pl.ds(0, 3)], v.sw.at[pl.ds(0, 3 * skr)])):
+        remote(ref, ref, v.mid_s.at[kind], v.mid_r.at[0], r, mate).wait_send()
     moved = (share - ALONE) * UNIT
     level = r // 2
     for count in range(1, R // 2):
@@ -1102,7 +1152,7 @@
 
     all_of(v.fp.at[pl.ds(0, R // 2), pl.ds(0, moved)], 8).wait_send()
     all_of(v.fp.at[pl.ds(0, R - 1), pl.ds(0, ALONE * UNIT)], 9).wait_send()
-    all_of(mate_rows, 10).wait_send()
+    all_of(v.fp.at[pl.ds(0, R - 1), pl.ds(0, share * UNIT)], 10).wait_send()
 
 
 def fast_shards(
@@ -1137,6 +1187,7 @@
         hx=pltpu.VMEM((CP // LANES, N + 16, LANES), F32),
         ox=pltpu.VMEM((CP // LANES, N + 16, LANES), F32),
         act_a=pltpu.VMEM((3, N + 16, 2 * C), BF16), act_b=pltpu.VMEM((3, N, 2 * C), BF16),
+        act_c=pltpu.VMEM((N + 16, 3 * C), BF16), act_d=pltpu.VMEM((N, 3 * C), BF16),
         front_v=pltpu.VMEM((C, fk), BF16), fw=pltpu.VMEM((18 * C, CP), BF16),
         fp=pltpu.VMEM((R, PACK * UNIT, 2 * C), BF16), mp=pltpu.VMEM((Q, PACK * UNIT, 2 * C), BF16),
         mid_v=pltpu.VMEM((C, mk), BF16), mw=pltpu.VMEM((9 * C, CP), BF16),
@@ -1149,7 +1200,7 @@
         gain_one=pltpu.VMEM((2 * C,), F32), gain_two=pltpu.VMEM((C,), F32),
         gain_three=pltpu.VMEM((C,), F32),
         ld_s=dma((13,)), one_s=dma((11,)), one_r=dma((11,)), halo_s=dma((3, 2)), halo_r=dma((3, 2)),
-        fm_r=dma((2, R)), fx_r=dma((R,)), mid_s=dma((12,)), mid_r=dma((12,)),
+        fm_r=dma((2, R)), fx_r=dma((R,)), fo_r=dma((R,)), mid_s=dma((2,)), mid_r=dma((12,)),
         sum_s=dma((3,)), sum_r=dma((3,)),
     )
     specs = [hbm] * len(args)

time: 51.9 us -> 51.1 us (0.985)
  Pallas kernels: 49.7 us -> 48.9 us
    pallas_call x1, Pallas kernels: 49.7 us -> 48.9 us  [fast_shards(): pl.pallas_call(functools.partial(fast_kernel, R, Q, tuple(shapes)), out_s...]
where the time goes in v2:
time: 51.1 us; the launch traced here: 50.9 us
  Pallas kernels  48.9 us (96%)
  local copies, waits for them, and re-layouts  1.28 us (3%)
  between operations  0.66 us (1%)
    pallas_call x1, Pallas kernels, fast_shards(): pl.pallas_call(functools.partial(fast_kernel, R, Q, tuple(shapes)), out_s...  48.9 us
    reshape x1, local copies, waits for them, and re-layouts, fast_shards(): return out.reshape(couts, 1, px)  1.28 us

profile of v2, /device:TPU:0, one launch (start us, length us, event | category | flops | bytes accessed | tf_op | source)
XLA Modules:
  0.0 50.9 jit_solution(5221573975766754333)
XLA Ops:
  0.7 48.9 %shard_map.136 = f32[4,256]{1,0:T(4,128)} custom-call(bf16[4,256]{1,0:T(4,128)(2,1)} %bitcast.13, bf16[320,256]{1,0:T(8,128)(2,1)} %bitcast.10, s32[1]{0:T(128)S(6)} %copy.16.timestep, bf16[36,320]{1,0:T(8,128)(2,1)} %in_w.1, bf16[320,720]{1,0:T(8,128)(2,1)} %bitcast.8, bf16[320,720]{1,0:T(8,128)(2,1)} %bitcast.9, bf16[160,320]{1,0:T(8,128)(2,1)} %skip.1, ...), custom_call_target="tpu_custom_call" | custom-call | tf_op jit(solution)/shard_map/pallas_call | solution.py:1208
  49.6 1.3 %copy.15 = f32[4,1,256]{2,1,0:T(1,128)} copy(f32[4,1,256]{2,0,1:T(4,128)} %bitcast.12) | data formatting | bytes 8192 | tf_op jit(solution)/shard_map/reshape | solution.py:1218

commit v3 on v2

--- a/solution.py
+++ b/solution.py
@@ -543,11 +543,14 @@
     main = C // LANES * LANES
     tail = C - main
 
+    def side_by_side(first, second):
+        mixed = jnp.concatenate([first[:, main:C], second[:, main:C]], axis=1)
+        return jnp.concatenate([first[:, 0:main], mixed, second[:, 0:main]], axis=1).astype(BF16)
+
     def packed(ref, k):
         turned = ref[...].astype(F32).T
         first, second = turned[0:tall], turned[k - tall : k]
-        mixed = jnp.concatenate([first[:, main:C], second[:, main:C]], axis=1)
-        return jnp.concatenate([first[:, 0:main], mixed, second[:, 0:main]], axis=1).astype(BF16)
+        return side_by_side(first, second)
 
     def unpack(block, ref, start):
         def at(first):
@@ -599,7 +602,7 @@
     sizes = (ALONE, share - 2 * ALONE)
 
     def f_part(owner, part, x_of, core_of):
-        first = (x_of * (share - ALONE), ALONE)[part]
+        first = (x_of * (share - ALONE), ALONE, share // 2)[part]
         return v.fp.at[owner, pl.ds(
             pl.multiple_of((core_of * share + first) * UNIT, UNIT), sizes[part] * UNIT)]
 
@@ -633,7 +636,7 @@
         def _():
             body()
 
-    for part in (0, 1):
+    for part in range(2):
         when_row(r + 2, lambda: f_up(r, part).start())
         when_row(r - 2, lambda: f_down(r, part).start())
         f_twin(r, part).start()
@@ -669,12 +672,12 @@
             when_row(t, lambda: from_x(t + twins * (twin - r)))
 
     def z_steps(d):
-        for part in (0, 1):
+        for part in range(2):
             for sign in (-1, 1):
                 from_z(d, sign, part)
 
     def y_steps(d):
-        for part in (0, 1):
+        for part in range(2):
             for sign in (-1, 1):
                 t = r + sign * 2 * d
                 when_row(t, lambda: from_y(t + twin - r, part))
@@ -716,13 +719,15 @@
 
     loads["deep"].wait()
     deep_t = v.deep_v[...].astype(F32).T
-    v.dr[:, C:CP] = jnp.zeros((px, GAP), BF16)
-    v.dr[:, 0:C] = deep_t.astype(BF16)
+    halves = deep_t.reshape(R, 2, W // 2, C)
+    doubled = side_by_side(halves[:, 0].reshape(px // 2, C), halves[:, 1].reshape(px // 2, C))
+    for q in range(R):
+        v.dr[q] = doubled[W // 2 * q : W // 2 * (q + 1)]
     pad = jnp.zeros((1, GAP), F32)
     deep_top = jnp.concatenate([jnp.sum(deep_t, axis=0, keepdims=True), pad], axis=1)
     deep_low = jnp.concatenate([jnp.sum(deep_t * deep_t, axis=0, keepdims=True), pad], axis=1)
     def a2a_copy(q):
-        return remote(v.dr.at[pl.ds(W * q, W)], v.a2a.at[r], v.one_s.at[3], v.one_r.at[3],
+        return remote(v.dr.at[q], v.a2a.at[r], v.one_s.at[3], v.one_r.at[3],
                       snake(q, c, R), c)
 
     def a2a_send():
@@ -733,7 +738,7 @@
 
             @pl.when(s == q)
             def _():
-                v.a2a[r] = v.dr[pl.ds(W * q, W), :]
+                v.a2a[r] = v.dr[q]
 
     unpack(v.fp[r], v.fw, r * fk)
 
@@ -898,7 +903,7 @@
             halo_left(stage, ext).wait_recv()
 
     z_steps(1)
-    for part in (0, 1):
+    for part in range(2):
         from_y(twin, part)
     z_steps(2)
     a2a_send()
@@ -909,7 +914,14 @@
         y_steps(d - 1)
     all_of(v.a2a.at[pl.ds(0, R - 1)], 3).wait_recv()
     for q in range(R):
-        joined = join(v.a2a[q].astype(F32), v.sk[:, q * CP : (q + 1) * CP])
+        block = v.a2a[q].astype(F32)
+        mixed = block[:, main : main + LANES]
+        used = lax.broadcasted_iota(jnp.int32, mixed.shape, 1) < tail
+        upper = jnp.concatenate([block[:, 0:main], jnp.where(used, mixed, 0.0)], axis=1)
+        lower = jnp.concatenate(
+            [block[:, main + LANES : 2 * C],
+             jnp.where(used, pltpu.roll(mixed, LANES - tail, 1), 0.0)], axis=1)
+        joined = join(jnp.concatenate([upper, lower], axis=0), v.sk[:, q * CP : (q + 1) * CP])
         for n in range(2 * C // LANES):
             v.jx[n, pl.ds(8 + q, W, 8), :] = joined[:, n * LANES : (n + 1) * LANES]
     halo_send(0, v.jx)
@@ -1181,7 +1193,7 @@
     shapes = dict(
         lat_v=pltpu.VMEM((cin, px), BF16), lat=pltpu.VMEM((3, R, cin, px), BF16),
         latrows=pltpu.VMEM((3, R * cin, px), F32), deep_v=pltpu.VMEM((C, px), BF16),
-        dr=pltpu.VMEM((px, CP), BF16), a2a=pltpu.VMEM((R, W, CP), BF16),
+        dr=pltpu.VMEM((R, W // 2, 2 * C), BF16), a2a=pltpu.VMEM((R, W // 2, 2 * C), BF16),
         inw=pltpu.VMEM((9 * cin, C), BF16), wb=pltpu.VMEM((3, R * cin, R * CP), F32),
         sk=pltpu.VMEM((W, R * CP), F32), jx=pltpu.VMEM((2 * C // LANES, N + 16, LANES), F32),
         hx=pltpu.VMEM((CP // LANES, N + 16, LANES), F32),
@@ -1200,7 +1212,7 @@
         gain_one=pltpu.VMEM((2 * C,), F32), gain_two=pltpu.VMEM((C,), F32),
         gain_three=pltpu.VMEM((C,), F32),
         ld_s=dma((13,)), one_s=dma((11,)), one_r=dma((11,)), halo_s=dma((3, 2)), halo_r=dma((3, 2)),
-        fm_r=dma((2, R)), fx_r=dma((R,)), fo_r=dma((R,)), mid_s=dma((2,)), mid_r=dma((12,)),
+        fm_r=dma((3, R)), fx_r=dma((R,)), fo_r=dma((R,)), mid_s=dma((2,)), mid_r=dma((12,)),
         sum_s=dma((3,)), sum_r=dma((3,)),
     )
     specs = [hbm] * len(args)

time: 51.1 us -> 50.8 us (level)
  no operation moved by 1% of the time
where the time goes in v3:
time: 50.8 us; the launch traced here: 50.6 us
  Pallas kernels  48.7 us (96%)
  local copies, waits for them, and re-layouts  1.28 us (3%)
  between operations  0.66 us (1%)
    pallas_call x1, Pallas kernels, fast_shards(): pl.pallas_call(functools.partial(fast_kernel, R, Q, tuple(shapes)), out_s...  48.7 us
    reshape x1, local copies, waits for them, and re-layouts, fast_shards(): return out.reshape(couts, 1, px)  1.28 us

profile of v3, /device:TPU:0, one launch (start us, length us, event | category | flops | bytes accessed | tf_op | source)
XLA Modules:
  0.0 50.6 jit_solution(10310932439739644907)
XLA Ops:
  0.7 48.7 %shard_map.136 = f32[4,256]{1,0:T(4,128)} custom-call(bf16[4,256]{1,0:T(4,128)(2,1)} %bitcast.13, bf16[320,256]{1,0:T(8,128)(2,1)} %bitcast.10, s32[1]{0:T(128)S(6)} %copy.16.timestep, bf16[36,320]{1,0:T(8,128)(2,1)} %in_w.1, bf16[320,720]{1,0:T(8,128)(2,1)} %bitcast.8, bf16[320,720]{1,0:T(8,128)(2,1)} %bitcast.9, bf16[160,320]{1,0:T(8,128)(2,1)} %skip.1, ...), custom_call_target="tpu_custom_call" | custom-call | tf_op jit(solution)/shard_map/pallas_call | solution.py:1220
  49.3 1.3 %copy.15 = f32[4,1,256]{2,1,0:T(1,128)} copy(f32[4,1,256]{2,0,1:T(4,128)} %bitcast.12) | data formatting | bytes 8192 | tf_op jit(solution)/shard_map/reshape | solution.py:1230

commit v4 on v3

--- a/solution.py
+++ b/solution.py
@@ -905,9 +905,9 @@
     z_steps(1)
     for part in range(2):
         from_y(twin, part)
+    mid_over(1, c).start()
     z_steps(2)
     a2a_send()
-    mid_over(1, c).start()
     y_steps(1)
     for d in range(3, R // 2):
         z_steps(d)

time: 50.8 us -> 50.8 us (level)
  no operation moved by 1% of the time
where the time goes in v4:
time: 50.8 us; the launch traced here: 50.6 us
  Pallas kernels  48.7 us (96%)
  local copies, waits for them, and re-layouts  1.28 us (3%)
  between operations  0.66 us (1%)
    pallas_call x1, Pallas kernels, fast_shards(): pl.pallas_call(functools.partial(fast_kernel, R, Q, tuple(shapes)), out_s...  48.7 us
    reshape x1, local copies, waits for them, and re-layouts, fast_shards(): return out.reshape(couts, 1, px)  1.28 us

profile of v4, /device:TPU:0, one launch (start us, length us, event | category | flops | bytes accessed | tf_op | source)
XLA Modules:
  0.0 50.6 jit_solution(1129958635655403352)
XLA Ops:
  0.7 48.7 %shard_map.136 = f32[4,256]{1,0:T(4,128)} custom-call(bf16[4,256]{1,0:T(4,128)(2,1)} %bitcast.13, bf16[320,256]{1,0:T(8,128)(2,1)} %bitcast.10, s32[1]{0:T(128)S(6)} %copy.16.timestep, bf16[36,320]{1,0:T(8,128)(2,1)} %in_w.1, bf16[320,720]{1,0:T(8,128)(2,1)} %bitcast.8, bf16[320,720]{1,0:T(8,128)(2,1)} %bitcast.9, bf16[160,320]{1,0:T(8,128)(2,1)} %skip.1, ...), custom_call_target="tpu_custom_call" | custom-call | tf_op jit(solution)/shard_map/pallas_call | solution.py:1220
  49.3 1.3 %copy.15 = f32[4,1,256]{2,1,0:T(1,128)} copy(f32[4,1,256]{2,0,1:T(4,128)} %bitcast.12) | data formatting | bytes 8192 | tf_op jit(solution)/shard_map/reshape | solution.py:1230
